TPU v7x, 32 devices: a whole 2x2x4 slice. The times are simulated.
32 devices in a mesh: fsdp: 2 (over y), ctx: 4 (over x, core), tp: 4 (over z).
Axes of the slice: x: 2, y: 2, z: 4, core: 2. Of those that a mesh axis runs over, the one named last changes fastest.
Arguments:
- block_input: bfloat16 [4, 2048, 1024], P('fsdp', 'ctx'), may hold values from -6 to 6
- positions: int32 [3, 4, 2048], P(None, 'fsdp', 'ctx'), may hold values from 0 to 15
- w_qkv: bfloat16 [3, 1024, 1024], P(None, 'fsdp', 'tp'), may hold values from -0.1875 to 0.1875
- b_qkv: float32 [3, 1024], P(None, 'tp'), may hold values from -3 to 3
- w_proj: bfloat16 [1024, 1024], P('tp', 'fsdp'), may hold values from -1 to 1
- w_up: bfloat16 [1024, 4096], P('fsdp', 'tp'), may hold values from -0.1875 to 0.1875
- b_up: float32 [4096], P('tp'), may hold values from -3 to 3
- w_down: bfloat16 [4096, 1024], P('tp', 'fsdp'), may hold values from -0.09375 to 0.09375
- norm_gains: float32 [2, 1024], replicated, may hold values from 0.5 to 1.5
- norm_shifts: float32 [2, 1024], replicated, may hold values from -2 to 2
- out_shifts: float32 [2, 1024], replicated, may hold values from -2 to 2
- grad_out: bfloat16 [4, 2048, 1024], P('fsdp', 'ctx'), may hold values from -6 to 6
Outputs:
- block_output: bfloat16 [4, 2048, 1024], P('fsdp', 'ctx')
- grad_input: float32 [4, 2048, 1024], P('fsdp', 'ctx')
- grad_w_qkv: float32 [3, 1024, 1024], P(None, 'fsdp', 'tp')
- grad_b_qkv: float32 [3, 1024], P(None, 'tp')
- grad_w_proj: float32 [1024, 1024], P('tp', 'fsdp')
- grad_w_up: float32 [1024, 4096], P('fsdp', 'tp')
- grad_b_up: float32 [4096], P('tp')
- grad_w_down: float32 [4096, 1024], P('tp', 'fsdp')
- grad_gains: float32 [2, 1024], replicated
- grad_shifts: float32 [2, 1024], replicated
- grad_out_shifts: float32 [2, 1024], replicated
Inputs may be any that keep to these rules, and one draw needn't show every extreme that they name: `positions`: each token's time, height and width index in its clip.
All inputs are finite; a program needn't handle non-finite values.
Results may differ from a plain program's by a relative error of at most 0.02.
Values may be sent and summed in bfloat16 or wider, within the bound.
A program may use at most 128 MiB of HBM per device.

v0:
```python
from functools import partial
import jax
import jax.numpy as jnp
from jax import lax
from jax.sharding import PartitionSpec as P

HD = 64
LEN = 2048
ROT = 20
QBLK = 512
EPSILON = 1e-06


def layer_norm(values, gain_vec, shift_vec):
    center = values - jnp.mean(values, axis=-1, keepdims=True)
    spread = jnp.mean(center * center, axis=-1, keepdims=True)
    return center * lax.rsqrt(spread + EPSILON) * gain_vec + shift_vec


def rotary_tables(position_rows):
    half_rot = ROT // 2
    freqs = 10000.0 ** (-2.0 * jnp.arange(half_rot, dtype=jnp.float32) / ROT)
    angles = position_rows.astype(jnp.float32)[:, :, None] * freqs[None, None, :]
    return (jnp.cos(angles), jnp.sin(angles))


def rotary(values, cos_table, sin_table):
    half_rot = ROT // 2
    pieces = []
    for dim_index in range(3):
        offset_at = dim_index * ROT
        first_half = values[..., offset_at : offset_at + half_rot]
        second_half = values[..., offset_at + half_rot : offset_at + ROT]
        cos_part = cos_table[dim_index][:, None, :]
        sin_part = sin_table[dim_index][:, None, :]
        pieces.append(first_half * cos_part - second_half * sin_part)
        pieces.append(second_half * cos_part + first_half * sin_part)
    pieces.append(values[..., 3 * ROT :])
    return jnp.concatenate(pieces, axis=-1)


def contract_rows(left_mat, right_mat):
    return lax.dot_general(
        left_mat, right_mat, (((0,), (0,)), ((), ())), preferred_element_type=jnp.float32
    )


def contract_cols(left_mat, right_mat):
    return lax.dot_general(
        left_mat, right_mat, (((1,), (1,)), ((), ())), preferred_element_type=jnp.float32
    )


def tp_whole(partial_sum):
    return lax.psum(partial_sum.astype(jnp.bfloat16), "tp").astype(jnp.float32)


def attend_group(operands):
    queries, keys_all, values_all = operands
    score_factor = HD ** (-0.5)

    def attend_block(query_block):
        scores = (
            jnp.einsum("qe,ke->qk", query_block, keys_all, preferred_element_type=jnp.float32)
            * score_factor
        )
        largest = jnp.max(scores, axis=-1, keepdims=True)
        expon = jnp.exp(scores - largest)
        totals = jnp.sum(expon, axis=-1, keepdims=True)
        probs = expon / totals
        block_out = jnp.dot(
            probs.astype(jnp.bfloat16), values_all, preferred_element_type=jnp.float32
        )
        return (block_out.astype(jnp.bfloat16), (largest + jnp.log(totals))[:, 0])

    return lax.map(attend_block, queries.reshape(LEN // QBLK, QBLK, HD))


def backward_group(operands):
    queries, keys_all, values_all, grad_attended, log_totals = operands
    score_factor = HD ** (-0.5)

    def back_block(carry, block_items):
        grad_keys, grad_values = carry
        query_block, grad_block, log_block = block_items
        scores = (
            jnp.einsum("qe,ke->qk", query_block, keys_all, preferred_element_type=jnp.float32)
            * score_factor
        )
        probs = jnp.exp(scores - log_block[:, None])
        probs_low = probs.astype(jnp.bfloat16)
        grad_probs = jnp.einsum(
            "qe,ke->qk", grad_block, values_all, preferred_element_type=jnp.float32
        )
        inner = jnp.sum(probs * grad_probs, axis=-1, keepdims=True)
        grad_scores = (probs * (grad_probs - inner)).astype(jnp.bfloat16)
        grad_query = (
            jnp.dot(grad_scores, keys_all, preferred_element_type=jnp.float32) * score_factor
        )
        grad_keys = grad_keys + contract_rows(grad_scores, query_block) * score_factor
        grad_values = grad_values + contract_rows(probs_low, grad_block)
        return ((grad_keys, grad_values), grad_query)

    zeros_kv = jnp.zeros((LEN, HD), jnp.float32)
    block_count = LEN // QBLK
    items = (
        queries.reshape(block_count, QBLK, HD),
        grad_attended.reshape(block_count, QBLK, HD),
        log_totals,
    )
    (grad_keys, grad_values), grad_queries = lax.scan(back_block, (zeros_kv, zeros_kv), items)
    return (grad_queries.reshape(LEN, HD), grad_keys, grad_values)


def shards(
    block_input,
    positions,
    w_qkv,
    b_qkv,
    w_proj,
    w_up,
    b_up,
    w_down,
    norm_gains,
    norm_shifts,
    out_shifts,
    grad_out,
):
    clip_count, local_len, width = block_input.shape
    row_count = clip_count * local_len
    ctx_count = lax.axis_size("ctx")
    local_width = w_qkv.shape[2]
    group_heads = local_width // ctx_count // HD
    group_count = clip_count * group_heads
    inputs = block_input.reshape(row_count, width).astype(jnp.float32)
    full_qkv, full_proj, full_up, full_down = (
        lax.all_gather(w_qkv, "fsdp", axis=1, tiled=True),
        lax.all_gather(w_proj, "fsdp", axis=1, tiled=True),
        lax.all_gather(w_up, "fsdp", axis=0, tiled=True),
        lax.all_gather(w_down, "fsdp", axis=1, tiled=True),
    )
    cos_table, sin_table = rotary_tables(positions.reshape(3, row_count))
    normed_one = layer_norm(inputs, norm_gains[0], norm_shifts[0])
    normed_one_low = normed_one.astype(jnp.bfloat16)
    projected = (
        jnp.einsum("rd,cde->cre", normed_one_low, full_qkv, preferred_element_type=jnp.float32)
        + b_qkv[:, None, :]
    )
    head_shape = (row_count, local_width // HD, HD)
    queries_rot = rotary(projected[0].reshape(head_shape), cos_table, sin_table).reshape(
        row_count, local_width
    )
    keys_rot = rotary(projected[1].reshape(head_shape), cos_table, sin_table).reshape(
        row_count, local_width
    )
    token_qkv = (
        jnp.stack([queries_rot, keys_rot, projected[2]])
        .astype(jnp.bfloat16)
        .reshape(3, clip_count, local_len, local_width)
    )
    head_qkv = lax.all_to_all(token_qkv, "ctx", split_axis=3, concat_axis=2, tiled=True)
    full_len = head_qkv.shape[2]
    grouped = (
        head_qkv.reshape(3, clip_count, full_len, group_heads, HD)
        .transpose(0, 1, 3, 2, 4)
        .reshape(3, group_count, full_len, HD)
    )
    attended, log_totals = lax.map(attend_group, (grouped[0], grouped[1], grouped[2]))
    attended = (
        attended.reshape(clip_count, group_heads, full_len, HD)
        .transpose(0, 2, 1, 3)
        .reshape(clip_count, full_len, group_heads * HD)
    )
    token_attended = lax.all_to_all(
        attended, "ctx", split_axis=1, concat_axis=2, tiled=True
    ).reshape(row_count, local_width)
    attn_part = jnp.dot(token_attended, full_proj, preferred_element_type=jnp.float32)
    residual = inputs + tp_whole(attn_part) + out_shifts[0]
    normed_two_low = layer_norm(residual, norm_gains[1], norm_shifts[1]).astype(jnp.bfloat16)
    pre_act = jnp.dot(normed_two_low, full_up, preferred_element_type=jnp.float32) + b_up
    act_low = jax.nn.gelu(pre_act, approximate=False).astype(jnp.bfloat16)
    mlp_part = jnp.dot(act_low, full_down, preferred_element_type=jnp.float32)
    result = residual + tp_whole(mlp_part) + out_shifts[1]
    block_rows = result.astype(jnp.bfloat16)
    full_qkv, full_proj, full_up, full_down = (
        lax.all_gather(w_qkv, "fsdp", axis=1, tiled=True),
        lax.all_gather(w_proj, "fsdp", axis=1, tiled=True),
        lax.all_gather(w_up, "fsdp", axis=0, tiled=True),
        lax.all_gather(w_down, "fsdp", axis=1, tiled=True),
    )
    upstream = grad_out.reshape(row_count, width).astype(jnp.float32)
    upstream_low = upstream.astype(jnp.bfloat16)
    grad_down = contract_rows(act_low, upstream_low)
    grad_act = contract_cols(upstream_low, full_down)
    _, gelu_pull = jax.vjp(partial(jax.nn.gelu, approximate=False), pre_act)
    grad_pre = gelu_pull(grad_act)[0].astype(jnp.bfloat16)
    grad_b_up = jnp.sum(grad_pre.astype(jnp.float32), axis=0)
    grad_up = contract_rows(normed_two_low, grad_pre)
    back_part_two = contract_cols(grad_pre, full_up)
    grad_normed_two = tp_whole(back_part_two)
    _, norm_pull_two = jax.vjp(layer_norm, residual, norm_gains[1], norm_shifts[1])
    grad_res_norm, grad_gain_two, grad_shift_two = norm_pull_two(grad_normed_two)
    grad_residual = upstream + grad_res_norm
    grad_residual_low = grad_residual.astype(jnp.bfloat16)
    grad_proj = contract_rows(token_attended, grad_residual_low)
    grad_token_att = (
        contract_cols(grad_residual_low, full_proj)
        .astype(jnp.bfloat16)
        .reshape(clip_count, local_len, local_width)
    )
    grad_head_att = lax.all_to_all(grad_token_att, "ctx", split_axis=2, concat_axis=1, tiled=True)
    grad_grouped = (
        grad_head_att.reshape(clip_count, full_len, group_heads, HD)
        .transpose(0, 2, 1, 3)
        .reshape(group_count, full_len, HD)
    )
    grad_q, grad_k, grad_v = lax.map(
        backward_group, (grouped[0], grouped[1], grouped[2], grad_grouped, log_totals)
    )
    grad_heads = jnp.stack([grad_q, grad_k, grad_v]).astype(jnp.bfloat16)
    grad_heads = (
        grad_heads.reshape(3, clip_count, group_heads, full_len, HD)
        .transpose(0, 1, 3, 2, 4)
        .reshape(3, clip_count, full_len, group_heads * HD)
    )
    grad_tokens = (
        lax.all_to_all(grad_heads, "ctx", split_axis=2, concat_axis=3, tiled=True)
        .reshape(3, row_count, local_width)
        .astype(jnp.float32)
    )

    def rotate_rows(moved):
        return rotary(moved, cos_table, sin_table)

    _, rotary_pull = jax.vjp(rotate_rows, jnp.zeros(head_shape, jnp.float32))
    grad_q_pre = rotary_pull(grad_tokens[0].reshape(head_shape))[0].reshape(row_count, local_width)
    grad_k_pre = rotary_pull(grad_tokens[1].reshape(head_shape))[0].reshape(row_count, local_width)
    grad_qkv_low = jnp.stack([grad_q_pre, grad_k_pre, grad_tokens[2]]).astype(jnp.bfloat16)
    grad_b_qkv = jnp.sum(grad_qkv_low.astype(jnp.float32), axis=1)
    grad_qkv = jnp.einsum(
        "rd,cre->cde", normed_one_low, grad_qkv_low, preferred_element_type=jnp.float32
    )
    back_part_one = jnp.einsum(
        "cre,cde->rd", grad_qkv_low, full_qkv, preferred_element_type=jnp.float32
    )
    grad_normed_one = tp_whole(back_part_one)
    _, norm_pull_one = jax.vjp(layer_norm, inputs, norm_gains[0], norm_shifts[0])
    grad_in_norm, grad_gain_one, grad_shift_one = norm_pull_one(grad_normed_one)
    grad_input_rows = grad_residual + grad_in_norm
    norm_vectors = jnp.stack(
        [
            grad_gain_one,
            grad_gain_two,
            grad_shift_one,
            grad_shift_two,
            jnp.sum(grad_residual, axis=0),
            jnp.sum(upstream, axis=0),
        ]
    )
    block_output = block_rows.reshape(clip_count, local_len, width)
    grad_input = grad_input_rows.reshape(clip_count, local_len, width)
    shard_qkv, shard_proj, shard_up, shard_down = (
        lax.psum_scatter(
            grad_qkv.astype(jnp.bfloat16), "fsdp", scatter_dimension=1, tiled=True
        ).astype(jnp.float32),
        lax.psum_scatter(
            grad_proj.astype(jnp.bfloat16), "fsdp", scatter_dimension=1, tiled=True
        ).astype(jnp.float32),
        lax.psum_scatter(
            grad_up.astype(jnp.bfloat16), "fsdp", scatter_dimension=0, tiled=True
        ).astype(jnp.float32),
        lax.psum_scatter(
            grad_down.astype(jnp.bfloat16), "fsdp", scatter_dimension=1, tiled=True
        ).astype(jnp.float32),
    )
    shard_qkv, shard_proj, shard_up, shard_down = (
        lax.psum(shard_qkv.astype(jnp.bfloat16), "ctx").astype(jnp.float32),
        lax.psum(shard_proj.astype(jnp.bfloat16), "ctx").astype(jnp.float32),
        lax.psum(shard_up.astype(jnp.bfloat16), "ctx").astype(jnp.float32),
        lax.psum(shard_down.astype(jnp.bfloat16), "ctx").astype(jnp.float32),
    )
    gains_sum, shifts_sum, outs_sum, bqkv_sum, bup_sum = lax.psum(
        (norm_vectors[0:2], norm_vectors[2:4], norm_vectors[4:6], grad_b_qkv, grad_b_up),
        ("fsdp", "ctx"),
    )
    return (
        block_output,
        grad_input,
        shard_qkv,
        bqkv_sum,
        shard_proj,
        shard_up,
        bup_sum,
        shard_down,
        gains_sum,
        shifts_sum,
        outs_sum,
    )


def solution(mesh):
    in_specs = (
        P("fsdp", "ctx", None),
        P(None, "fsdp", "ctx"),
        P(None, "fsdp", "tp"),
        P(None, "tp"),
        P("tp", "fsdp"),
        P("fsdp", "tp"),
        P("tp"),
        P("tp", "fsdp"),
        P(),
        P(),
        P(),
        P("fsdp", "ctx", None),
    )
    out_specs = (
        P("fsdp", "ctx", None),
        P("fsdp", "ctx", None),
        P(None, "fsdp", "tp"),
        P(None, "tp"),
        P("tp", "fsdp"),
        P("fsdp", "tp"),
        P("tp"),
        P("tp", "fsdp"),
        P(),
        P(),
        P(),
    )
    return jax.shard_map(shards, mesh=mesh, in_specs=in_specs, out_specs=out_specs, check_vma=False)
```

profile of v0, /device:TPU:0, one launch (start us, length us, event | category | flops | bytes accessed | tf_op | source)
XLA Modules:
  0.0 875.1 jit_solution(13437522062420596701)
XLA Ops:
  17.3 22.8 %all-gather.4.cloned.1.call-done = bf16[3,1024,256]{1,2,0:T(8,128)(2,1)} async-done(((bf16[3,512,256]{1,2,0:T(8,128)(2,1)}), bf16[3,1024,256]{1,2,0:T(8,128)(2,1)}) %all-gather.4.cloned.1.call-update) | async-done | bytes 1572880 | tf_op jit(solution)/shard_map/all_gather | solution.py:137
  40.1 3.9 add_bitcast_fusion
  51.5 3.1 pad_maximum_fusion.1
  54.5 3.8 all-to-all-start
  58.3 20.0 %all-to-all-done = bf16[3,2,512,256]{2,1,0,3:T(2,128)(2,1)S(1)} async-done(((bf16[3,2,512,256]{2,1,0,3:T(2,128)(2,1)}), bf16[3,2,512,256]{2,1,0,3:T(2,128)(2,1)S(1)}, u32[]{:S(2)}, u32[]{:S(2)}) %all-to-all-start) | async-done | bytes 1572896 | tf_op jit(solution)/shard_map/all_to_all | solution.py:161
  83.0 27.2 %while.54 = (s32[]{:T(128)}, bf16[2,4,512,64]{2,3,1,0:T(8,128)(2,1)}, f32[2,4,512]{2,1,0:T(4,128)S(1)}, bf16[2,2048,64]{2,1,0:T(8,128)(2,1)S(1)}, bf16[2,2048,64...) while((s32[]{:T(128)}, ...), condition=%wide.region_7.8_spmd, body=%wide.region_2.7_spmd.sunk | while | flops 277904896 | bytes 20156772 | solution.py:168
  84.4 11.4 %while.57 = (s32[]{:T(128)}, bf16[4,512,64]{1,2,0:T(8,128)(2,1)S(1)}, f32[4,512]{1,0:T(4,128)S(1)}, bf16[4,512,64]{2,1,0:T(8,128)(2,1)S(1)}, bf16[2048,64]{1,0:T...) while((s32[]{:T(128)}, bf16[4,512,64]{1,2,0:T(8,128)(2,1)S(1)}, ...), condition=%wide.region_6.6_spmd, body=%wide.region_3.5_spmd.sunk | while | flops 277904896 | bytes 13848681 | solution.py:76
  98.0 11.4 %while.57 = (s32[]{:T(128)}, bf16[4,512,64]{1,2,0:T(8,128)(2,1)S(1)}, f32[4,512]{1,0:T(4,128)S(1)}, bf16[4,512,64]{2,1,0:T(8,128)(2,1)S(1)}, bf16[2048,64]{1,0:T...) while((s32[]{:T(128)}, bf16[4,512,64]{1,2,0:T(8,128)(2,1)S(1)}, ...), condition=%wide.region_6.6_spmd, body=%wide.region_3.5_spmd.sunk | while | flops 277904896 | bytes 13848681 | solution.py:76
  114.4 3.5 all-to-all-start.1
  117.9 9.3 %all_gather.17 = bf16[256,1024]{1,0:T(8,128)(2,1)S(1)} all-gather(bf16[256,512]{1,0:T(8,128)(2,1)S(1)} %copy-done.30), channel_id=1, replica_groups=mesh['fsdp'=2,'ctx'=4,'tp'=4] {'fsdp'}, dimensions={1}, use_global_device_ids=true | all-gather | bytes 786432 | tf_op jit(solution)/shard_map/all_gather | solution.py:138
  135.5 84.2 %all-reduce.22.cloned.1.call-done = bf16[1024,1024]{1,0:T(8,128)(2,1)} async-done(((bf16[1024,1024]{1,0:T(8,128)(2,1)}), bf16[1024,1024]{1,0:T(8,128)(2,1)}) %all-reduce.22.cloned.1.call-update) | async-done | bytes 2097168 | tf_op jit(solution)/shard_map/psum | solution.py:55
  222.2 3.0 multiply_reduce_fusion.2
  225.3 28.2 %all-gather.6.cloned.1.call-done = bf16[1024,1024]{1,0:T(8,128)(2,1)} async-done(((bf16[512,1024]{1,0:T(8,128)(2,1)}), bf16[1024,1024]{1,0:T(8,128)(2,1)}) %all-gather.6.cloned.1.call-update) | async-done | bytes 2097168 | tf_op jit(solution)/shard_map/all_gather | solution.py:139
  253.4 7.4 fusion.69
  260.8 27.1 %all-gather.8.cloned.1.call-done = bf16[1024,1024]{1,0:T(8,128)(2,1)} async-done(((bf16[1024,512]{1,0:T(8,128)(2,1)}), bf16[1024,1024]{1,0:T(8,128)(2,1)}) %all-gather.8.cloned.1.call-update) | async-done | bytes 2097168 | tf_op jit(solution)/shard_map/all_gather | solution.py:140
  287.9 16.0 %convert_reduce_fusion.4 = (f32[1024]{0:T(1024)}, bf16[1024,1024]{1,0:T(8,128)(2,1)S(1)}, f32[1024,1024]{1,0:T(8,128)}) fusion(f32[1024,1024]{1,0:T(8,128)} %fusion.69, f32[1024]{0:T(1024)S(1)} %copy-done.50, bf16[1024,1024]{1,0:T(8,128)(2,1)S(1)} %bitcast.274, bf16[1024,1024]{1,0:T(8,128)(2,1)} %all-gather.8.cloned.1.call-done), kind=kOutput, calls=%fused_computation.82 | convolution fusion | flops 2226125824 | bytes 14688256 | tf_op jit(solution)/shard_map/dot_general | solution.py:49
  305.2 3.7 convolution_convert_fusion.2
  308.9 12.1 %reduce-scatter.7.cloned.1.call-start = ((), (), s32[]{:S(2)}) async-start(), calls=%async_computation.14 | async-start | bytes 786432 | tf_op jit(solution)/shard_map/reduce_scatter | solution.py:266
  321.1 74.2 %all-reduce.24.cloned.1.call-done = bf16[1024,1024]{1,0:T(8,128)(2,1)} async-done(((bf16[1024,1024]{1,0:T(8,128)(2,1)}), bf16[1024,1024]{1,0:T(8,128)(2,1)}) %all-reduce.24.cloned.1.call-update) | async-done | bytes 2097168 | tf_op jit(solution)/shard_map/psum | solution.py:55
  395.3 4.5 convert_reduce_fusion.1
  408.6 4.6 multiply_convert_fusion.1
  414.5 3.8 convolution_convert_fusion
  418.3 3.0 convolution_convert_fusion.6
  422.5 3.5 all-to-all-start.2
  426.0 6.9 convolution_convert_fusion.1
  436.1 103.6 %while.56 = (s32[]{:T(128)}, bf16[2,2048,64]{2,0,1:T(2,128)(2,1)}, bf16[2,2048,64]{1,2,0:T(8,128)(2,1)}, bf16[2,2048,64]{1,2,0:T(8,128)(2,1)}, bf16[2,2048,64]{2...) while((s32[]{:T(128)}, bf16[2,2048,64]{2,0,1:T(2,128)(2,1)}, ...), condition=%wide.region_19.20_spmd, body=%wide.region_15.19_spmd.sunk | while | flops 680164864 | bytes 41838996 | solution.py:217
  440.5 20.1 %while.58 = (s32[]{:T(128)}, f32[2048,64]{0,1:T(8,128)S(1)}, f32[2048,64]{0,1:T(8,128)S(1)}, f32[4,512,64]{1,2,0:T(8,128)}, bf16[4,512,64]{2,1,0:T(8,128)(2,1)S(...) while((s32[]{:T(128)}, f32[2048,64]{0,1:T(8,128)S(1)}, ...), condition=%wide.region_18.18_spmd.clone, body=%wide.region_16.17_spmd.clone.sunk | while | flops 680164864 | bytes 35530900 | solution.py:111
  462.0 25.1 %dynamic_update_slice.47 = bf16[2,2048,64]{2,0,1:T(2,128)(2,1)} dynamic-update-slice(bf16[2,2048,64]{2,0,1:T(2,128)(2,1)} %get-tuple-element.795, f32[1,2048,64]{2,0,1:T(1,128)S(1)} %bitcast.268, s32[]{:T(128)S(6)} %copy.189, s32[]{:T(128)} %constant.78.clone.1..sunk.2, s32[]{:T(128)} %constant.78.clone.1..sunk.2) | dynamic-update-slice | bytes 1048580 | tf_op jit(solution)/shard_map/while/body/jit(dynamic_update_index_in_dim)/dynamic_update_slice | solution.py:217
  492.3 20.1 %while.58 = (s32[]{:T(128)}, f32[2048,64]{0,1:T(8,128)S(1)}, f32[2048,64]{0,1:T(8,128)S(1)}, f32[4,512,64]{1,2,0:T(8,128)}, bf16[4,512,64]{2,1,0:T(8,128)(2,1)S(...) while((s32[]{:T(128)}, f32[2048,64]{0,1:T(8,128)S(1)}, ...), condition=%wide.region_18.18_spmd.clone, body=%wide.region_16.17_spmd.clone.sunk | while | flops 680164864 | bytes 35530900 | solution.py:111
  513.8 25.1 %dynamic_update_slice.47 = bf16[2,2048,64]{2,0,1:T(2,128)(2,1)} dynamic-update-slice(bf16[2,2048,64]{2,0,1:T(2,128)(2,1)} %get-tuple-element.795, f32[1,2048,64]{2,0,1:T(1,128)S(1)} %bitcast.268, s32[]{:T(128)S(6)} %copy.189, s32[]{:T(128)} %constant.78.clone.1..sunk.2, s32[]{:T(128)} %constant.78.clone.1..sunk.2) | dynamic-update-slice | bytes 1048580 | tf_op jit(solution)/shard_map/while/body/jit(dynamic_update_index_in_dim)/dynamic_update_slice | solution.py:217
  539.7 3.6 copy.142
  543.3 3.6 copy.141
  546.8 7.2 fusion.79
  554.0 3.3 reshape.228
  557.3 24.7 %all_to_all.57 = bf16[4,2,98304]{2,1,0:T(2,128)(2,1)} all-to-all(bf16[4,2,98304]{2,1,0:T(2,128)(2,1)} %reshape.228), channel_id=1, replica_groups=mesh['fsdp'=2,'ctx'=4,'tp'=4] {'ctx'}, dimensions={0} | all-to-all | bytes 3145728 | tf_op jit(solution)/shard_map/all_to_all | solution.py:227
  582.0 3.8 reshape.229
  585.8 6.4 copy.92
  601.3 4.9 fusion.61
  606.3 5.4 convolution_convert_fusion.3
  611.7 3.1 bitcast_convert_fusion
  618.7 11.9 %reduce-scatter.5.cloned.1.call-done = bf16[3,512,256]{1,2,0:T(8,128)(2,1)} async-done(((bf16[3,1024,256]{1,2,0:T(8,128)(2,1)}), bf16[3,512,256]{1,2,0:T(8,128)(2,1)}) %reduce-scatter.5.cloned.1.call-update) | async-done | bytes 786448 | tf_op jit(solution)/shard_map/reduce_scatter | solution.py:263
  630.7 157.9 %all-reduce.26.cloned.1.call-done = (bf16[1024,1024]{1,0:T(8,128)(2,1)}, bf16[1024,1024]{1,0:T(8,128)(2,1)}) async-done(((bf16[1024,1024]{1,0:T(8,128)(2,1)}, bf16[1024,1024]{1,0:T(8,128)(2,1)}), (bf16[1024,1024]{1,0:T(8,128)(2,1)}, bf16[1024,1024]{1,0:T(8,128)(2,1)})) %all-reduce.26.cloned.1.call-update) | async-done | bytes 4194320 | tf_op jit(solution)/shard_map/psum | solution.py:55
  788.6 3.1 convert_reduce_fusion
  791.7 2.7 fusion.35
  794.5 26.2 %all-reduce.14 = (f32[3,256]{1,0:T(4,128)}, f32[1024]{0:T(1024)}, f32[2,1024]{1,0:T(2,128)}, f32[2,1024]{1,0:T(2,128)}, f32[2,1024]{1,0:T(2,128)}) all-reduce(f32[3,256]{1,0:T(4,128)S(1)} %convert_reduce_fusion.5, f32[1024]{0:T(1024)S(1)} %copy-done.52, ...), channel_id=1, replica_groups=mesh['fsdp'=2,'ctx'=4,'tp'=4] {'fsdp','ctx'}, use_global_device_ids=true, to_apply=%region_26.27 | all-reduce | flops 7936 | bytes 63488 | tf_op jit(solution)/shard_map/psum | solution.py:282
  820.7 7.1 add_add_fusion.2
  827.9 31.4 %all-reduce.28.cloned.1.call-done = (bf16[3,512,256]{1,2,0:T(8,128)(2,1)}, bf16[256,512]{1,0:T(8,128)(2,1)}, bf16[512,1024]{1,0:T(8,128)(2,1)}, bf16[1024,512]{1,0:T(8,128)(2,1)}) async-done(((bf16[3,512,256]{1,2,0:T(8,128)(2,1)}, bf16[256,512]{1,0:T(8,128)(2,1)}, bf16[512,1024]{1,0:T(8,128)(2,1)}, bf16[1024,512]{1,0:T(8,128)(2,1)}), (bf16[3,512,256]{1,2,0:T(8,128)(2,1)}, bf16[256,512]{1,0:T(8,128)(2,1)}, ...) | async-done | bytes 3145744 | tf_op jit(solution)/shard_map/psum | solution.py:277
  863.7 2.8 convert_element_type.170
  (351 shorter events, 151.5 us)
Async XLA Ops:
  7.2 5.3 copy-start.46
  7.2 5.8 copy-start.47
  7.2 6.4 copy-start.48
  7.2 32.9 %all-gather.4.cloned.1.call-start = ((), (), s32[]{:S(2)}) async-start(), calls=%async_computation.8 | async-start | bytes 2359296 | tf_op jit(solution)/shard_map/all_gather | solution.py:137
  11.7 28.4 %copy-start.55 = (f32[3,256]{1,0:T(4,128)S(1)}, f32[3,256]{1,0:T(4,128)}, u32[]{:S(2)}) copy-start(f32[3,256]{1,0:T(4,128)} %param.23) | copy-start | bytes 9220
  15.0 30.8 %copy-start.15 = (f32[1024,10]{0,1:T(8,128)}, f32[1024,10]{0,1:T(8,128)S(1)}, u32[]{:S(2)}) copy-start(f32[1024,10]{0,1:T(8,128)S(1)} %get-tuple-element.436) | copy-start | bytes 122884
  15.0 30.8 %copy-start.17 = (f32[1024,10]{0,1:T(8,128)}, f32[1024,10]{0,1:T(8,128)S(1)}, u32[]{:S(2)}) copy-start(f32[1024,10]{0,1:T(8,128)S(1)} %get-tuple-element.437) | copy-start | bytes 122884
  15.0 30.8 %copy-start.19 = (f32[1024,10]{0,1:T(8,128)}, f32[1024,10]{0,1:T(8,128)S(1)}, u32[]{:S(2)}) copy-start(f32[1024,10]{0,1:T(8,128)S(1)} %get-tuple-element.438) | copy-start | bytes 122884
  15.1 30.8 %copy-start.21 = (f32[1024,10]{0,1:T(8,128)}, f32[1024,10]{0,1:T(8,128)S(1)}, u32[]{:S(2)}) copy-start(f32[1024,10]{0,1:T(8,128)S(1)} %get-tuple-element.449) | copy-start | bytes 122884
  15.1 30.8 %copy-start.23 = (f32[1024,10]{0,1:T(8,128)}, f32[1024,10]{0,1:T(8,128)S(1)}, u32[]{:S(2)}) copy-start(f32[1024,10]{0,1:T(8,128)S(1)} %get-tuple-element.450) | copy-start | bytes 122884
  15.1 30.8 %copy-start.25 = (f32[1024,10]{0,1:T(8,128)}, f32[1024,10]{0,1:T(8,128)S(1)}, u32[]{:S(2)}) copy-start(f32[1024,10]{0,1:T(8,128)S(1)} %get-tuple-element.451) | copy-start | bytes 122884
  54.5 23.8 %all-to-all-start = ((bf16[3,2,512,256]{2,1,0,3:T(2,128)(2,1)}), bf16[3,2,512,256]{2,1,0,3:T(2,128)(2,1)S(1)}, u32[]{:S(2)}, u32[]{:S(2)}) async-start(bf16[3,2,512,256]{2,1,0,3:T(2,128)(2,1)} %pad_maximum_fusion.1), calls=%async_computation | async-start | bytes 3145728 | tf_op jit(solution)/shard_map/all_to_all | solution.py:161
  84.4 11.4 %copy-start.28 = (bf16[2,4,512,64]{2,3,1,0:T(8,128)(2,1)S(1)}, bf16[2,4,512,64]{2,3,1,0:T(8,128)(2,1)}, u32[]{:S(2)}) copy-start(bf16[2,4,512,64]{2,3,1,0:T(8,128)(2,1)} %get-tuple-element.762) | copy-start | bytes 1572868 | tf_op jit(solution)/shard_map/while
  98.0 11.4 %copy-start.28 = (bf16[2,4,512,64]{2,3,1,0:T(8,128)(2,1)S(1)}, bf16[2,4,512,64]{2,3,1,0:T(8,128)(2,1)}, u32[]{:S(2)}) copy-start(bf16[2,4,512,64]{2,3,1,0:T(8,128)(2,1)} %get-tuple-element.762) | copy-start | bytes 1572868 | tf_op jit(solution)/shard_map/while
  110.2 19.6 %copy-start.5 = (bf16[2,2048,64]{2,1,0:T(8,128)(2,1)}, bf16[2,2048,64]{2,1,0:T(8,128)(2,1)S(1)}, u32[]{:S(2)}) copy-start(bf16[2,2048,64]{2,1,0:T(8,128)(2,1)S(1)} %get-tuple-element.841) | copy-start | bytes 1572868
  110.3 7.7 copy-start.30
  114.4 12.8 %all-to-all-start.1 = ((bf16[4,2,32768]{2,1,0:T(2,128)(2,1)}), bf16[4,2,32768]{2,1,0:T(2,128)(2,1)S(1)}, u32[]{:S(2)}, u32[]{:S(2)}) async-start(bf16[4,2,32768]{2,1,0:T(2,128)(2,1)} %reshape.226), calls=%async_computation.1 | async-start | bytes 1048576 | tf_op jit(solution)/shard_map/all_to_all | solution.py:174
  117.9 101.8 %all-reduce.22.cloned.1.call-start = ((), (), s32[]{:S(2)}) async-start(), calls=%async_computation.9 | async-start | bytes 4194304 | tf_op jit(solution)/shard_map/psum | solution.py:55
  129.9 89.8 %copy-start.1 = (bf16[2,512,1024]{2,1,0:T(8,128)(2,1)S(1)}, bf16[2,512,1024]{2,1,0:T(8,128)(2,1)}, u32[]{:S(2)}) copy-start(bf16[2,512,1024]{2,1,0:T(8,128)(2,1)} %param.20) | copy-start | bytes 6291460
  133.2 120.2 %all-gather.6.cloned.1.call-start = ((), (), s32[]{:S(2)}) async-start(), calls=%async_computation.10 | async-start | bytes 3145728 | tf_op jit(solution)/shard_map/all_gather | solution.py:139
  134.0 154.0 %all-gather.8.cloned.1.call-start = ((), (), s32[]{:S(2)}) async-start(), calls=%async_computation.11 | async-start | bytes 3145728 | tf_op jit(solution)/shard_map/all_gather | solution.py:140
  134.5 260.7 %all-reduce.24.cloned.1.call-start = ((), (), s32[]{:S(2)}) async-start(), calls=%async_computation.12 | async-start | bytes 4194304 | tf_op jit(solution)/shard_map/psum | solution.py:55
  135.5 89.7 %copy-start.36 = (f32[1,1024]{1,0:T(1,128)}, f32[1,1024]{1,0:T(1,128)S(1)}, u32[]{:S(2)}) copy-start(f32[1,1024]{1,0:T(1,128)S(1)} %get-tuple-element.442) | copy-start | bytes 12292
  222.2 31.2 %copy-start.35 = (f32[1,1024]{1,0:T(1,128)S(1)}, f32[1,1024]{1,0:T(1,128)}, u32[]{:S(2)}) copy-start(f32[1,1024]{1,0:T(1,128)} %get-tuple-element.443) | copy-start | bytes 12292
  222.2 31.2 %copy-start.51 = (f32[1,1024]{1,0:T(1,128)S(1)}, f32[1,1024]{1,0:T(1,128)}, u32[]{:S(2)}) copy-start(f32[1,1024]{1,0:T(1,128)} %get-tuple-element.445) | copy-start | bytes 12292
  253.4 34.5 %copy-start.10 = (bf16[2,512,1024]{2,1,0:T(8,128)(2,1)S(1)}, bf16[2,512,1024]{2,1,0:T(8,128)(2,1)}, u32[]{:S(2)}) copy-start(bf16[2,512,1024]{2,1,0:T(8,128)(2,1)} %param.31) | copy-start | bytes 6291460
  253.4 34.5 %copy-start.50 = (f32[1024]{0:T(1024)S(1)}, f32[1024]{0:T(1024)}, u32[]{:S(2)}) copy-start(f32[1024]{0:T(1024)} %param.26) | copy-start | bytes 12292
  287.9 17.3 %copy-start.53 = (bf16[1024,1024]{1,0:T(8,128)(2,1)S(1)}, bf16[1024,1024]{1,0:T(8,128)(2,1)}, u32[]{:S(2)}) copy-start(bf16[1024,1024]{1,0:T(8,128)(2,1)} %all-gather.6.cloned.1.call-done) | copy-start | bytes 6291460
  308.9 309.7 %reduce-scatter.7.cloned.1.call-start = ((), (), s32[]{:S(2)}) async-start(), calls=%async_computation.14 | async-start | bytes 786432 | tf_op jit(solution)/shard_map/reduce_scatter | solution.py:266
  408.5 210.2 %reduce-scatter.11.cloned.1.call-start = ((), (), s32[]{:S(2)}) async-start(), calls=%async_computation.16 | async-start | bytes 3145728 | tf_op jit(solution)/shard_map/reduce_scatter | solution.py:272
  422.5 12.3 %all-to-all-start.2 = ((bf16[2,512,256]{1,0,2:T(2,128)(2,1)}), bf16[2,512,256]{1,0,2:T(2,128)(2,1)S(1)}, u32[]{:S(2)}, u32[]{:S(2)}) async-start(bf16[2,512,256]{1,0,2:T(2,128)(2,1)} %copy.83), calls=%async_computation.2 | async-start | bytes 1048576 | tf_op jit(solution)/shard_map/all_to_all | solution.py:211
  426.0 192.7 %reduce-scatter.9.cloned.1.call-start = ((), (), s32[]{:S(2)}) async-start(), calls=%async_computation.15 | async-start | bytes 3145728 | tf_op jit(solution)/shard_map/reduce_scatter | solution.py:269
  432.9 197.7 %reduce-scatter.5.cloned.1.call-start = ((), (), s32[]{:S(2)}) async-start(), calls=%async_computation.13 | async-start | bytes 2359296 | tf_op jit(solution)/shard_map/reduce_scatter | solution.py:263
  606.2 182.3 %all-reduce.26.cloned.1.call-start = ((), (), s32[]{:S(2)}) async-start(), calls=%async_computation.17 | async-start | bytes 8388608 | tf_op jit(solution)/shard_map/psum | solution.py:55
  606.3 5.4 copy-start.14
  606.3 5.4 copy-start.54
  614.8 173.7 %copy-start.2 = (bf16[2,512,1024]{2,1,0:T(8,128)(2,1)S(1)}, bf16[2,512,1024]{2,1,0:T(8,128)(2,1)}, u32[]{:S(2)}) copy-start(bf16[2,512,1024]{2,1,0:T(8,128)(2,1)} %param.20) | copy-start | bytes 6291460
  614.8 173.7 %copy-start.32 = (f32[1,4,2,128]{3,1,2,0:T(4,128)S(1)}, f32[1,4,2,128]{3,1,2,0:T(4,128)}, u32[]{:S(2)}) copy-start(f32[1,4,2,128]{3,1,2,0:T(4,128)} %copy-done.31) | copy-start | bytes 12292
  614.9 173.7 %copy-start.34 = (f32[1,1024]{1,0:T(1,128)S(1)}, f32[1,1024]{1,0:T(1,128)}, u32[]{:S(2)}) copy-start(f32[1,1024]{1,0:T(1,128)} %copy-done.33) | copy-start | bytes 12292
  614.9 244.4 %all-reduce.28.cloned.1.call-start = ((), (), s32[]{:S(2)}) async-start(), calls=%async_computation.18 | async-start | bytes 6291456 | tf_op jit(solution)/shard_map/psum | solution.py:277
  617.3 174.4 %copy-start.41 = (f32[1,4,2,128]{3,1,2,0:T(4,128)S(1)}, f32[1,4,2,128]{3,1,2,0:T(4,128)}, u32[]{:S(2)}) copy-start(f32[1,4,2,128]{3,1,2,0:T(4,128)} %copy-done.40) | copy-start | bytes 12292
  617.3 174.4 %copy-start.44 = (f32[1024]{0:T(1024)S(1)}, f32[1024]{0:T(1024)}, u32[]{:S(2)}) copy-start(f32[1024]{0:T(1024)} %get-tuple-element.296) | copy-start | bytes 12292
  617.3 174.4 %copy-start.39 = (f32[1024]{0:T(1024)S(1)}, f32[1024]{0:T(1024)}, u32[]{:S(2)}) copy-start(f32[1024]{0:T(1024)} %copy-done.38) | copy-start | bytes 12292
  788.5 5.9 copy-start.43
  788.5 5.9 copy-start.52
  788.6 32.2 %copy-start.37 = (f32[1,1024]{1,0:T(1,128)S(1)}, f32[1,1024]{1,0:T(1,128)}, u32[]{:S(2)}) copy-start(f32[1,1024]{1,0:T(1,128)} %copy-done.36) | copy-start | bytes 12292
  788.6 32.2 %copy-start.45 = (f32[1,1024]{1,0:T(1,128)S(1)}, f32[1,1024]{1,0:T(1,128)}, u32[]{:S(2)}) copy-start(f32[1,1024]{1,0:T(1,128)} %get-tuple-element.441) | copy-start | bytes 12292
  859.2 7.2 copy-start.27
  (25 other events, 62.0 us)
Sparse Core Ops, SparseCore 0:
  10.1 29.8 all-gather.3
  133.3 86.3 all-reduce.21
  221.2 32.1 all-gather.5
  254.8 33.0 all-gather.7
  309.1 86.1 all-reduce.23
  408.7 13.6 reduce-scatter.6
  424.6 31.8 reduce-scatter.10
  458.8 31.8 reduce-scatter.8
  606.3 24.2 reduce-scatter.4
  633.5 155.0 all-reduce.25
  791.1 68.0 all-reduce.27
where the time goes:
time: 888 us; the launch traced here: 875 us
  waiting for transfers between devices  461 us (52%)
  local copies, waits for them, and re-layouts  130 us (15%)
  matrix products  113 us (13%)
  other arithmetic  71.1 us (8%)
  blocking collectives  60.2 us (7%)
  starting transfers between devices  23.8 us (3%)
  between operations  15.3 us (2%)
    psum x3, waiting for transfers between devices, tp_whole(): return lax.psum(partial_sum.astype(jnp.bfloat16), 'tp').astype(jnp.float32)  316 us
    dynamic_update_slice x4, local copies, waits for them, and re-layouts, shards(): lax.map(backward_group, (grouped[0], grouped[1], grouped[2], grad_grouped...  51.9 us
    psum x1, waiting for transfers between devices, shards(): lax.psum(shard_qkv.astype(jnp.bfloat16), 'ctx').astype(jnp.float32)  31.4 us
    unnamed x122, local copies, waits for them, and re-layouts  28.2 us
    all_gather x1, waiting for transfers between devices, shards(): lax.all_gather(w_up, 'fsdp', axis=0, tiled=True)  28.2 us
    all_gather x1, waiting for transfers between devices, shards(): lax.all_gather(w_down, 'fsdp', axis=1, tiled=True)  27.1 us
    psum x1, blocking collectives, shards(): lax.psum((norm_vectors[0:2], norm_vectors[2:4], norm_vectors[4:6], grad_b...  26.2 us
    all_to_all x1, blocking collectives, shards(): lax.all_to_all(grad_heads, 'ctx', split_axis=2, concat_axis=3, tiled=True)  24.7 us
  transfers between devices with their start and end apart: 14, of which 10 were waited for; matrix products, arithmetic and copies ran while one was open for 24% of the time, Pallas kernels for 0%

commit v1 on v0

--- a/solution.py
+++ b/solution.py
@@ -224,7 +224,15 @@
         .reshape(3, clip_count, full_len, group_heads * HD)
     )
     grad_tokens = (
-        lax.all_to_all(grad_heads, "ctx", split_axis=2, concat_axis=3, tiled=True)
+        jnp.concatenate(
+            lax.all_to_all(
+                jnp.stack(jnp.split(grad_heads, lax.psum(1, axis_name="ctx"), axis=2), 0),
+                axis_name="ctx",
+                split_axis=0,
+                concat_axis=0,
+            ),
+            3,
+        )
         .reshape(3, row_count, local_width)
         .astype(jnp.float32)
     )

time: 888 us -> 805 us (0.907)
  local copies, waits for them, and re-layouts: 130 us -> 64 us
    dynamic_update_slice x4 -> x6, local copies, waits for them, and re-layouts: 51.9 us -> 3.59 us  [shards(): lax.map(backward_group, (grouped[0], grouped[1], grouped[2], grad_grouped...]
    unnamed x122, local copies, waits for them, and re-layouts: 28.2 us -> 14.8 us
  transfers between devices with their start and end apart: 14 -> 14, of which waited for: 10 -> 10; matrix products, arithmetic and copies ran while one was open for 24% -> 16% of each run, Pallas kernels for 0% -> 0%
where the time goes in v1:
time: 805 us; the launch traced here: 797 us
  waiting for transfers between devices  462 us (57%)
  matrix products  110 us (14%)
  other arithmetic  64.8 us (8%)
  local copies, waits for them, and re-layouts  64 us (8%)
  blocking collectives  58.3 us (7%)
  starting transfers between devices  22.7 us (3%)
  between operations  15.3 us (2%)
    psum x3, waiting for transfers between devices, tp_whole(): return lax.psum(partial_sum.astype(jnp.bfloat16), 'tp').astype(jnp.float32)  317 us
    psum x1, waiting for transfers between devices, shards(): lax.psum(shard_qkv.astype(jnp.bfloat16), 'ctx').astype(jnp.float32)  31.4 us
    all_gather x1, waiting for transfers between devices, shards(): lax.all_gather(w_up, 'fsdp', axis=0, tiled=True)  28.2 us
    all_gather x1, waiting for transfers between devices, shards(): lax.all_gather(w_down, 'fsdp', axis=1, tiled=True)  27.1 us
    psum x1, blocking collectives, shards(): lax.psum((norm_vectors[0:2], norm_vectors[2:4], norm_vectors[4:6], grad_b...  26.2 us
    all_gather x1, waiting for transfers between devices, shards(): lax.all_gather(w_qkv, 'fsdp', axis=1, tiled=True)  22.9 us
    dot_general x3, matrix products, contract_cols(): lax.dot_general(left_mat, right_mat, (((1,), (1,)), ((), ())), preferred_...  22.7 us
    all_to_all x1, blocking collectives, shards(): lax.all_to_all(jnp.stack(jnp.split(grad_heads, lax.psum(1, axis_name='ctx...  22.7 us
  transfers between devices with their start and end apart: 14, of which 10 were waited for; matrix products, arithmetic and copies ran while one was open for 16% of the time, Pallas kernels for 0%

profile of v1, /device:TPU:0, one launch (start us, length us, event | category | flops | bytes accessed | tf_op | source)
XLA Modules:
  0.0 797.4 jit_solution(14894585414075408104)
XLA Ops:
  7.3 2.4 copy.75
  17.2 22.9 %all-gather.4.cloned.1.call-done = bf16[3,1024,256]{1,2,0:T(8,128)(2,1)} async-done(((bf16[3,512,256]{1,2,0:T(8,128)(2,1)}), bf16[3,1024,256]{1,2,0:T(8,128)(2,1)}) %all-gather.4.cloned.1.call-update) | async-done | bytes 1572880 | tf_op jit(solution)/shard_map/all_gather | solution.py:137
  40.1 3.9 add_bitcast_fusion
  51.4 3.1 pad_maximum_fusion
  54.5 3.8 all-to-all-start
  58.3 20.0 %all-to-all-done = bf16[3,2,512,256]{2,1,0,3:T(2,128)(2,1)S(1)} async-done(((bf16[3,2,512,256]{2,1,0,3:T(2,128)(2,1)}), bf16[3,2,512,256]{2,1,0,3:T(2,128)(2,1)S(1)}, u32[]{:S(2)}, u32[]{:S(2)}) %all-to-all-start) | async-done | bytes 1572896 | tf_op jit(solution)/shard_map/all_to_all | solution.py:161
  78.3 2.3 fusion.75
  85.7 28.9 %while.54 = (s32[]{:T(128)}, bf16[2,4,512,64]{2,3,1,0:T(8,128)(2,1)}, f32[2,4,512]{2,1,0:T(4,128)S(1)}, bf16[2,2048,64]{2,1,0:T(8,128)(2,1)}, bf16[2,2048,64]{2,...) while((s32[]{:T(128)}, ...), condition=%wide.region_7.8_spmd, body=%wide.region_2.7_spmd.sunk | while | flops 277904896 | bytes 20156772 | solution.py:168
  87.9 11.4 %while.57 = (s32[]{:T(128)}, bf16[4,512,64]{1,2,0:T(8,128)(2,1)S(1)}, f32[4,512]{1,0:T(4,128)S(1)}, bf16[4,512,64]{2,1,0:T(8,128)(2,1)S(1)}, bf16[2048,64]{1,0:T...) while((s32[]{:T(128)}, bf16[4,512,64]{1,2,0:T(8,128)(2,1)S(1)}, ...), condition=%wide.region_6.6_spmd, body=%wide.region_3.5_spmd.sunk | while | flops 277904896 | bytes 13848681 | solution.py:76
  102.4 11.4 %while.57 = (s32[]{:T(128)}, bf16[4,512,64]{1,2,0:T(8,128)(2,1)S(1)}, f32[4,512]{1,0:T(4,128)S(1)}, bf16[4,512,64]{2,1,0:T(8,128)(2,1)S(1)}, bf16[2048,64]{1,0:T...) while((s32[]{:T(128)}, bf16[4,512,64]{1,2,0:T(8,128)(2,1)S(1)}, ...), condition=%wide.region_6.6_spmd, body=%wide.region_3.5_spmd.sunk | while | flops 277904896 | bytes 13848681 | solution.py:76
  114.7 2.4 copy.103
  118.6 3.5 all-to-all-start.1
  122.2 9.4 %all_gather.17 = bf16[256,1024]{1,0:T(8,128)(2,1)} all-gather(bf16[256,512]{1,0:T(8,128)(2,1)S(1)} %copy-done.34), channel_id=1, replica_groups=mesh['fsdp'=2,'ctx'=4,'tp'=4] {'fsdp'}, dimensions={1}, use_global_device_ids=true | all-gather | bytes 786432 | tf_op jit(solution)/shard_map/all_gather | solution.py:138
  136.3 3.1 convolution_convert_fusion.4
  141.7 84.2 %all-reduce.22.cloned.1.call-done = bf16[1024,1024]{1,0:T(8,128)(2,1)} async-done(((bf16[1024,1024]{1,0:T(8,128)(2,1)}), bf16[1024,1024]{1,0:T(8,128)(2,1)}) %all-reduce.22.cloned.1.call-update) | async-done | bytes 2097168 | tf_op jit(solution)/shard_map/psum | solution.py:55
  225.8 2.5 fusion.50
  228.4 3.0 multiply_reduce_fusion.2
  231.4 28.2 %all-gather.6.cloned.1.call-done = bf16[1024,1024]{1,0:T(8,128)(2,1)} async-done(((bf16[512,1024]{1,0:T(8,128)(2,1)}), bf16[1024,1024]{1,0:T(8,128)(2,1)}) %all-gather.6.cloned.1.call-update) | async-done | bytes 2097168 | tf_op jit(solution)/shard_map/all_gather | solution.py:139
  259.6 7.4 fusion.69
  267.0 27.1 %all-gather.8.cloned.1.call-done = bf16[1024,1024]{1,0:T(8,128)(2,1)} async-done(((bf16[1024,512]{1,0:T(8,128)(2,1)}), bf16[1024,1024]{1,0:T(8,128)(2,1)}) %all-gather.8.cloned.1.call-update) | async-done | bytes 2097168 | tf_op jit(solution)/shard_map/all_gather | solution.py:140
  294.1 15.9 %convert_reduce_fusion.4 = (f32[1024]{0:T(1024)}, bf16[1024,1024]{1,0:T(8,128)(2,1)S(1)}, f32[1024,1024]{1,0:T(8,128)}) fusion(f32[1024,1024]{1,0:T(8,128)} %fusion.69, f32[1024]{0:T(1024)S(1)} %copy-done.54, bf16[1024,1024]{1,0:T(8,128)(2,1)S(1)} %bitcast.276, bf16[1024,1024]{1,0:T(8,128)(2,1)} %all-gather.8.cloned.1.call-done), kind=kOutput, calls=%fused_computation.83 | convolution fusion | flops 2226125824 | bytes 14688256 | tf_op jit(solution)/shard_map/dot_general | solution.py:49
  311.4 3.7 convolution_convert_fusion.2
  315.1 11.0 %reduce-scatter.7.cloned.1.call-start = ((), (), s32[]{:S(2)}) async-start(), calls=%async_computation.14 | async-start | bytes 786432 | tf_op jit(solution)/shard_map/reduce_scatter | solution.py:274
  326.1 75.3 %all-reduce.24.cloned.1.call-done = bf16[1024,1024]{1,0:T(8,128)(2,1)} async-done(((bf16[1024,1024]{1,0:T(8,128)(2,1)}), bf16[1024,1024]{1,0:T(8,128)(2,1)}) %all-reduce.24.cloned.1.call-update) | async-done | bytes 2097168 | tf_op jit(solution)/shard_map/psum | solution.py:55
  401.4 4.5 convert_reduce_fusion.1
  406.1 2.7 fusion.34
  408.8 2.4 fusion.70
  414.8 4.6 multiply_convert_fusion.1
  420.7 3.8 convolution_convert_fusion
  424.5 3.1 convolution_convert_fusion.6
  428.8 3.5 all-to-all-start.2
  432.3 6.9 convolution_convert_fusion.1
  442.4 47.7 %while.56 = (s32[]{:T(128)}, bf16[2,2048,64]{1,2,0:T(8,128)(2,1)}, bf16[2,2048,64]{1,2,0:T(8,128)(2,1)}, bf16[2,2048,64]{1,2,0:T(8,128)(2,1)}, bf16[2,2048,64]{2...) while((s32[]{:T(128)}, bf16[2,2048,64]{1,2,0:T(8,128)(2,1)}, ...), condition=%wide.region_19.20_spmd, body=%wide.region_15.19_spmd.sunk | while | flops 680164864 | bytes 45771212 | solution.py:217
  446.7 17.5 %while.58 = (s32[]{:T(128)}, f32[2048,64]{0,1:T(8,128)S(1)}, f32[2048,64]{0,1:T(8,128)S(1)}, bf16[4,512,64]{1,2,0:T(8,128)(2,1)S(1)}, bf16[4,512,64]{2,1,0:T(8,1...) while((s32[]{:T(128)}, f32[2048,64]{0,1:T(8,128)S(1)}, ...), condition=%wide.region_18.18_spmd.clone, body=%wide.region_16.17_spmd.clone.sunk | while | flops 680164864 | bytes 35793044 | solution.py:111
  470.6 17.5 %while.58 = (s32[]{:T(128)}, f32[2048,64]{0,1:T(8,128)S(1)}, f32[2048,64]{0,1:T(8,128)S(1)}, bf16[4,512,64]{1,2,0:T(8,128)(2,1)S(1)}, bf16[4,512,64]{2,1,0:T(8,1...) while((s32[]{:T(128)}, f32[2048,64]{0,1:T(8,128)S(1)}, ...), condition=%wide.region_18.18_spmd.clone, body=%wide.region_16.17_spmd.clone.sunk | while | flops 680164864 | bytes 35793044 | solution.py:111
  492.0 22.7 %all_to_all.53 = bf16[4,3,2,512,64]{3,4,2,1,0:T(8,128)(2,1)S(1)} all-to-all(bf16[4,3,2,512,64]{3,4,2,1,0:T(8,128)(2,1)S(1)} %pad_maximum_fusion.2), channel_id=1, replica_groups=mesh['fsdp'=2,'ctx'=4,'tp'=4] {'ctx'}, dimensions={0} | all-to-all | bytes 3145728 | tf_op jit(solution)/shard_map/all_to_all | solution.py:228
  523.4 5.1 fusion.61
  528.7 5.4 convolution_convert_fusion.3
  534.1 3.1 bitcast_convert_fusion
  541.1 11.8 %reduce-scatter.5.cloned.1.call-done = bf16[3,512,256]{1,2,0:T(8,128)(2,1)} async-done(((bf16[3,1024,256]{1,2,0:T(8,128)(2,1)}), bf16[3,512,256]{1,2,0:T(8,128)(2,1)}) %reduce-scatter.5.cloned.1.call-update) | async-done | bytes 786448 | tf_op jit(solution)/shard_map/reduce_scatter | solution.py:271
  553.0 157.9 %all-reduce.26.cloned.1.call-done = (bf16[1024,1024]{1,0:T(8,128)(2,1)}, bf16[1024,1024]{1,0:T(8,128)(2,1)}) async-done(((bf16[1024,1024]{1,0:T(8,128)(2,1)}, bf16[1024,1024]{1,0:T(8,128)(2,1)}), (bf16[1024,1024]{1,0:T(8,128)(2,1)}, bf16[1024,1024]{1,0:T(8,128)(2,1)})) %all-reduce.26.cloned.1.call-update) | async-done | bytes 4194320 | tf_op jit(solution)/shard_map/psum | solution.py:55
  710.9 3.1 convert_reduce_fusion
  714.1 2.7 fusion.35
  716.8 26.2 %all-reduce.14 = (f32[3,256]{1,0:T(4,128)}, f32[1024]{0:T(1024)}, f32[2,1024]{1,0:T(2,128)}, f32[2,1024]{1,0:T(2,128)}, f32[2,1024]{1,0:T(2,128)}) all-reduce(f32[3,256]{1,0:T(4,128)S(1)} %convert_reduce_fusion.5, f32[1024]{0:T(1024)S(1)} %copy-done.56, ...), channel_id=1, replica_groups=mesh['fsdp'=2,'ctx'=4,'tp'=4] {'fsdp','ctx'}, use_global_device_ids=true, to_apply=%region_26.27 | all-reduce | flops 7936 | bytes 63488 | tf_op jit(solution)/shard_map/psum | solution.py:290
  743.1 7.1 add_add_fusion.2
  750.2 31.4 %all-reduce.28.cloned.1.call-done = (bf16[3,512,256]{1,2,0:T(8,128)(2,1)}, bf16[256,512]{1,0:T(8,128)(2,1)}, bf16[512,1024]{1,0:T(8,128)(2,1)}, bf16[1024,512]{1,0:T(8,128)(2,1)}) async-done(((bf16[3,512,256]{1,2,0:T(8,128)(2,1)}, bf16[256,512]{1,0:T(8,128)(2,1)}, bf16[512,1024]{1,0:T(8,128)(2,1)}, bf16[1024,512]{1,0:T(8,128)(2,1)}), (bf16[3,512,256]{1,2,0:T(8,128)(2,1)}, bf16[256,512]{1,0:T(8,128)(2,1)}, ...) | async-done | bytes 3145744 | tf_op jit(solution)/shard_map/psum | solution.py:285
  783.5 2.5 copy.100
  786.0 2.8 convert_element_type.166
  (364 shorter events, 132.9 us)
Async XLA Ops:
  7.2 5.8 copy-start.51
  7.2 6.4 copy-start.52
  7.2 32.9 %all-gather.4.cloned.1.call-start = ((), (), s32[]{:S(2)}) async-start(), calls=%async_computation.8 | async-start | bytes 2359296 | tf_op jit(solution)/shard_map/all_gather | solution.py:137
  11.7 28.4 %copy-start.59 = (f32[3,256]{1,0:T(4,128)S(1)}, f32[3,256]{1,0:T(4,128)}, u32[]{:S(2)}) copy-start(f32[3,256]{1,0:T(4,128)} %param.23) | copy-start | bytes 9220
  11.7 32.3 %copy-start.35 = (f32[1,4,2,128]{3,1,2,0:T(4,128)}, f32[1,4,2,128]{3,1,2,0:T(4,128)S(1)}, u32[]{:S(2)}) copy-start(f32[1,4,2,128]{3,1,2,0:T(4,128)S(1)} %copy.141) | copy-start | bytes 12292
  12.5 31.5 %copy-start.42 = (f32[1024]{0:T(1024)}, f32[1024]{0:T(1024)S(1)}, u32[]{:S(2)}) copy-start(f32[1024]{0:T(1024)S(1)} %rsqrt.22) | copy-start | bytes 12292
  13.6 30.3 %copy-start.37 = (f32[1,1024]{1,0:T(1,128)}, f32[1,1024]{1,0:T(1,128)S(1)}, u32[]{:S(2)}) copy-start(f32[1,1024]{1,0:T(1,128)S(1)} %get-tuple-element.448) | copy-start | bytes 12292
  15.0 30.8 %copy-start.19 = (f32[1024,10]{0,1:T(8,128)}, f32[1024,10]{0,1:T(8,128)S(1)}, u32[]{:S(2)}) copy-start(f32[1024,10]{0,1:T(8,128)S(1)} %get-tuple-element.440) | copy-start | bytes 122884
  15.0 30.8 %copy-start.21 = (f32[1024,10]{0,1:T(8,128)}, f32[1024,10]{0,1:T(8,128)S(1)}, u32[]{:S(2)}) copy-start(f32[1024,10]{0,1:T(8,128)S(1)} %get-tuple-element.441) | copy-start | bytes 122884
  15.1 30.8 %copy-start.23 = (f32[1024,10]{0,1:T(8,128)}, f32[1024,10]{0,1:T(8,128)S(1)}, u32[]{:S(2)}) copy-start(f32[1024,10]{0,1:T(8,128)S(1)} %get-tuple-element.442) | copy-start | bytes 122884
  15.1 30.8 %copy-start.25 = (f32[1024,10]{0,1:T(8,128)}, f32[1024,10]{0,1:T(8,128)S(1)}, u32[]{:S(2)}) copy-start(f32[1024,10]{0,1:T(8,128)S(1)} %get-tuple-element.453) | copy-start | bytes 122884
  15.1 30.8 %copy-start.27 = (f32[1024,10]{0,1:T(8,128)}, f32[1024,10]{0,1:T(8,128)S(1)}, u32[]{:S(2)}) copy-start(f32[1024,10]{0,1:T(8,128)S(1)} %get-tuple-element.454) | copy-start | bytes 122884
  15.1 30.8 %copy-start.29 = (f32[1024,10]{0,1:T(8,128)}, f32[1024,10]{0,1:T(8,128)S(1)}, u32[]{:S(2)}) copy-start(f32[1024,10]{0,1:T(8,128)S(1)} %get-tuple-element.455) | copy-start | bytes 122884
  54.5 23.8 %all-to-all-start = ((bf16[3,2,512,256]{2,1,0,3:T(2,128)(2,1)}), bf16[3,2,512,256]{2,1,0,3:T(2,128)(2,1)S(1)}, u32[]{:S(2)}, u32[]{:S(2)}) async-start(bf16[3,2,512,256]{2,1,0,3:T(2,128)(2,1)} %pad_maximum_fusion), calls=%async_computation | async-start | bytes 3145728 | tf_op jit(solution)/shard_map/all_to_all | solution.py:161
  87.9 11.4 %copy-start.32 = (bf16[2,4,512,64]{2,3,1,0:T(8,128)(2,1)S(1)}, bf16[2,4,512,64]{2,3,1,0:T(8,128)(2,1)}, u32[]{:S(2)}) copy-start(bf16[2,4,512,64]{2,3,1,0:T(8,128)(2,1)} %get-tuple-element.766) | copy-start | bytes 1572868 | tf_op jit(solution)/shard_map/while
  102.4 11.4 %copy-start.32 = (bf16[2,4,512,64]{2,3,1,0:T(8,128)(2,1)S(1)}, bf16[2,4,512,64]{2,3,1,0:T(8,128)(2,1)}, u32[]{:S(2)}) copy-start(bf16[2,4,512,64]{2,3,1,0:T(8,128)(2,1)} %get-tuple-element.766) | copy-start | bytes 1572868 | tf_op jit(solution)/shard_map/while
  114.7 7.5 copy-start.34
  118.6 12.9 %all-to-all-start.1 = ((bf16[4,2,32768]{2,1,0:T(2,128)(2,1)}), bf16[4,2,32768]{2,1,0:T(2,128)(2,1)S(1)}, u32[]{:S(2)}, u32[]{:S(2)}) async-start(bf16[4,2,32768]{2,1,0:T(2,128)(2,1)} %reshape.224), calls=%async_computation.1 | async-start | bytes 1048576 | tf_op jit(solution)/shard_map/all_to_all | solution.py:174
  122.1 103.7 %all-reduce.22.cloned.1.call-start = ((), (), s32[]{:S(2)}) async-start(), calls=%async_computation.9 | async-start | bytes 4194304 | tf_op jit(solution)/shard_map/psum | solution.py:55
  134.2 6.9 copy-start.53
  134.2 91.6 %copy-start.1 = (bf16[2,512,1024]{2,1,0:T(8,128)(2,1)S(1)}, bf16[2,512,1024]{2,1,0:T(8,128)(2,1)}, u32[]{:S(2)}) copy-start(bf16[2,512,1024]{2,1,0:T(8,128)(2,1)} %param.20) | copy-start | bytes 6291460
  139.4 120.2 %all-gather.6.cloned.1.call-start = ((), (), s32[]{:S(2)}) async-start(), calls=%async_computation.10 | async-start | bytes 3145728 | tf_op jit(solution)/shard_map/all_gather | solution.py:139
  140.1 153.9 %all-gather.8.cloned.1.call-start = ((), (), s32[]{:S(2)}) async-start(), calls=%async_computation.11 | async-start | bytes 3145728 | tf_op jit(solution)/shard_map/all_gather | solution.py:140
  140.7 260.7 %all-reduce.24.cloned.1.call-start = ((), (), s32[]{:S(2)}) async-start(), calls=%async_computation.12 | async-start | bytes 4194304 | tf_op jit(solution)/shard_map/psum | solution.py:55
  141.7 89.7 %copy-start.40 = (f32[1,1024]{1,0:T(1,128)}, f32[1,1024]{1,0:T(1,128)S(1)}, u32[]{:S(2)}) copy-start(f32[1,1024]{1,0:T(1,128)S(1)} %get-tuple-element.446) | copy-start | bytes 12292
  228.4 31.2 %copy-start.39 = (f32[1,1024]{1,0:T(1,128)S(1)}, f32[1,1024]{1,0:T(1,128)}, u32[]{:S(2)}) copy-start(f32[1,1024]{1,0:T(1,128)} %get-tuple-element.447) | copy-start | bytes 12292
  228.4 31.2 %copy-start.55 = (f32[1,1024]{1,0:T(1,128)S(1)}, f32[1,1024]{1,0:T(1,128)}, u32[]{:S(2)}) copy-start(f32[1,1024]{1,0:T(1,128)} %get-tuple-element.449) | copy-start | bytes 12292
  259.6 34.5 %copy-start.10 = (bf16[2,512,1024]{2,1,0:T(8,128)(2,1)S(1)}, bf16[2,512,1024]{2,1,0:T(8,128)(2,1)}, u32[]{:S(2)}) copy-start(bf16[2,512,1024]{2,1,0:T(8,128)(2,1)} %param.31) | copy-start | bytes 6291460
  259.6 34.5 %copy-start.54 = (f32[1024]{0:T(1024)S(1)}, f32[1024]{0:T(1024)}, u32[]{:S(2)}) copy-start(f32[1024]{0:T(1024)} %param.26) | copy-start | bytes 12292
  294.1 17.3 %copy-start.57 = (bf16[1024,1024]{1,0:T(8,128)(2,1)S(1)}, bf16[1024,1024]{1,0:T(8,128)(2,1)}, u32[]{:S(2)}) copy-start(bf16[1024,1024]{1,0:T(8,128)(2,1)} %all-gather.6.cloned.1.call-done) | copy-start | bytes 6291460
  315.1 226.0 %reduce-scatter.7.cloned.1.call-start = ((), (), s32[]{:S(2)}) async-start(), calls=%async_computation.14 | async-start | bytes 786432 | tf_op jit(solution)/shard_map/reduce_scatter | solution.py:274
  414.7 126.4 %reduce-scatter.11.cloned.1.call-start = ((), (), s32[]{:S(2)}) async-start(), calls=%async_computation.16 | async-start | bytes 3145728 | tf_op jit(solution)/shard_map/reduce_scatter | solution.py:280
  428.8 12.3 %all-to-all-start.2 = ((bf16[2,512,256]{1,0,2:T(2,128)(2,1)}), bf16[2,512,256]{1,0,2:T(2,128)(2,1)S(1)}, u32[]{:S(2)}, u32[]{:S(2)}) async-start(bf16[2,512,256]{1,0,2:T(2,128)(2,1)} %copy.85), calls=%async_computation.2 | async-start | bytes 1048576 | tf_op jit(solution)/shard_map/all_to_all | solution.py:211
  432.3 108.8 %reduce-scatter.9.cloned.1.call-start = ((), (), s32[]{:S(2)}) async-start(), calls=%async_computation.15 | async-start | bytes 3145728 | tf_op jit(solution)/shard_map/reduce_scatter | solution.py:277
  439.2 113.7 %reduce-scatter.5.cloned.1.call-start = ((), (), s32[]{:S(2)}) async-start(), calls=%async_computation.13 | async-start | bytes 2359296 | tf_op jit(solution)/shard_map/reduce_scatter | solution.py:271
  528.6 182.3 %all-reduce.26.cloned.1.call-start = ((), (), s32[]{:S(2)}) async-start(), calls=%async_computation.17 | async-start | bytes 8388608 | tf_op jit(solution)/shard_map/psum | solution.py:55
  537.2 173.6 %copy-start.2 = (bf16[2,512,1024]{2,1,0:T(8,128)(2,1)S(1)}, bf16[2,512,1024]{2,1,0:T(8,128)(2,1)}, u32[]{:S(2)}) copy-start(bf16[2,512,1024]{2,1,0:T(8,128)(2,1)} %param.20) | copy-start | bytes 6291460
  537.2 173.6 %copy-start.36 = (f32[1,4,2,128]{3,1,2,0:T(4,128)S(1)}, f32[1,4,2,128]{3,1,2,0:T(4,128)}, u32[]{:S(2)}) copy-start(f32[1,4,2,128]{3,1,2,0:T(4,128)} %copy-done.35) | copy-start | bytes 12292
  537.2 173.6 %copy-start.38 = (f32[1,1024]{1,0:T(1,128)S(1)}, f32[1,1024]{1,0:T(1,128)}, u32[]{:S(2)}) copy-start(f32[1,1024]{1,0:T(1,128)} %copy-done.37) | copy-start | bytes 12292
  537.3 244.3 %all-reduce.28.cloned.1.call-start = ((), (), s32[]{:S(2)}) async-start(), calls=%async_computation.18 | async-start | bytes 6291456 | tf_op jit(solution)/shard_map/psum | solution.py:285
  539.7 174.3 %copy-start.45 = (f32[1,4,2,128]{3,1,2,0:T(4,128)S(1)}, f32[1,4,2,128]{3,1,2,0:T(4,128)}, u32[]{:S(2)}) copy-start(f32[1,4,2,128]{3,1,2,0:T(4,128)} %copy-done.44) | copy-start | bytes 12292
  539.7 174.3 %copy-start.48 = (f32[1024]{0:T(1024)S(1)}, f32[1024]{0:T(1024)}, u32[]{:S(2)}) copy-start(f32[1024]{0:T(1024)} %get-tuple-element.296) | copy-start | bytes 12292
  539.7 174.3 %copy-start.43 = (f32[1024]{0:T(1024)S(1)}, f32[1024]{0:T(1024)}, u32[]{:S(2)}) copy-start(f32[1024]{0:T(1024)} %copy-done.42) | copy-start | bytes 12292
  710.9 5.9 copy-start.47
  710.9 5.9 copy-start.56
  710.9 32.2 %copy-start.41 = (f32[1,1024]{1,0:T(1,128)S(1)}, f32[1,1024]{1,0:T(1,128)}, u32[]{:S(2)}) copy-start(f32[1,1024]{1,0:T(1,128)} %copy-done.40) | copy-start | bytes 12292
  710.9 32.2 %copy-start.49 = (f32[1,1024]{1,0:T(1,128)S(1)}, f32[1,1024]{1,0:T(1,128)}, u32[]{:S(2)}) copy-start(f32[1,1024]{1,0:T(1,128)} %get-tuple-element.445) | copy-start | bytes 12292
  781.6 7.2 copy-start.31
  (31 other events, 89.7 us)
Sparse Core Ops, SparseCore 0:
  10.1 29.8 all-gather.3
  139.5 86.2 all-reduce.21
  227.4 32.1 all-gather.5
  260.9 33.0 all-gather.7
  315.2 86.1 all-reduce.23
  414.8 13.6 reduce-scatter.6
  430.8 31.8 reduce-scatter.10
  465.0 31.8 reduce-scatter.8
  528.7 24.2 reduce-scatter.4
  555.8 155.0 all-reduce.25
  713.5 68.0 all-reduce.27
